TPU v7x, 32 devices: a whole 2x2x4 slice. The times are simulated.
32 devices in a mesh: shard: 8 (over y, x, core), tp: 4 (over z).
Axes of the slice: x: 2, y: 2, z: 4, core: 2. Of those that a mesh axis runs over, the one named last changes fastest.
Arguments:
- weight_gate: bfloat16 [2560, 9728], P('shard', 'tp'), may hold values from -0.15625 to 0.15625
- low_gate: bfloat16 [2560, 32], P('shard'), may hold values from -0.125 to 0.125
- high_gate: bfloat16 [32, 9728], P(None, 'tp'), may hold values from -1 to 1
- weight_up: bfloat16 [2560, 9728], P('shard', 'tp'), may hold values from -0.15625 to 0.15625
- low_up: bfloat16 [2560, 32], P('shard'), may hold values from -0.125 to 0.125
- high_up: bfloat16 [32, 9728], P(None, 'tp'), may hold values from -1 to 1
- norm_gain: float32 [2560], P('shard'), may hold values from 0.25 to 1.75
Outputs:
- ready_gate: bfloat16 [2560, 9728], P(None, 'tp')
- ready_up: bfloat16 [2560, 9728], P(None, 'tp')
- factor_gate: float32 [9728], P('tp')
- factor_up: float32 [9728], P('tp')
All inputs are finite; a program needn't handle non-finite values.
Results may differ from a plain program's by a relative error of at most 0.001.
Values may be sent and summed in bfloat16 or wider, within the bound.
A program may use at most 128 MiB of HBM per device.

v0:
```python
import jax
import jax.numpy as jnp
from jax import lax
from jax.sharding import PartitionSpec as P

mix_rate = 2.0


def local(weight_gate, low_gate, high_gate, weight_up, low_up, high_up, norm_gain):
    latest_gate = weight_gate.astype(jnp.float32) + mix_rate * jnp.dot(
        low_gate, high_gate, preferred_element_type=jnp.float32
    )
    latest_up = weight_up.astype(jnp.float32) + mix_rate * jnp.dot(
        low_up, high_up, preferred_element_type=jnp.float32
    )
    latest_gained_gate = latest_gate * norm_gain[:, None]
    latest_gained_up = latest_up * norm_gain[:, None]
    total_gate, total_up = lax.psum(
        (
            jnp.sum(latest_gained_gate * latest_gained_gate, axis=0),
            jnp.sum(latest_gained_up * latest_gained_up, axis=0),
        ),
        "shard",
    )
    factor_gate = jnp.sqrt(total_gate)
    factor_up = jnp.sqrt(total_up)
    narrow_gate, narrow_up = (
        (latest_gained_gate / factor_gate).astype(jnp.bfloat16),
        (latest_gained_up / factor_up).astype(jnp.bfloat16),
    )
    ready_gate, ready_up = (
        lax.all_gather(narrow_gate, "shard", axis=0, tiled=True),
        lax.all_gather(narrow_up, "shard", axis=0, tiled=True),
    )
    return (ready_gate, ready_up, factor_gate, factor_up)


def solution(mesh):
    in_specs = (
        P("shard", "tp"),
        P("shard", None),
        P(None, "tp"),
        P("shard", "tp"),
        P("shard", None),
        P(None, "tp"),
        P("shard"),
    )
    out_specs = (P(None, "tp"), P(None, "tp"), P("tp"), P("tp"))
    return jax.shard_map(local, mesh=mesh, in_specs=in_specs, out_specs=out_specs, check_vma=False)
```

profile of v0, /device:TPU:0, one launch (start us, length us, event | category | flops | bytes accessed | tf_op | source)
XLA Modules:
  0.0 211.0 jit_solution(10959377929472042755)
XLA Ops:
  7.2 0.0 copy-start
  7.2 0.0 copy-start.7
  7.2 0.0 copy-start.3
  7.2 0.0 copy-start.6
  7.2 0.0 all-gather.3.cloned.1.call-start
  7.3 0.8 copy-done
  8.1 0.0 copy-start.2
  8.1 4.0 %multiply_reduce_fusion.1 = (f32[2432]{0:T(1024)S(1)}, f32[320,2432]{1,0:T(8,128)}) fusion(f32[320]{0:T(512)} %param.13, bf16[320,32]{0,1:T(8,128)(2,1)} %param.8, bf16[32,2432]{1,0:T(8,128)(2,1)S(1)} %copy-done, bf16[320,2432]{1,0:T(8,128)(2,1)} %param.7), kind=kOutput, calls=%fused_computation.9 | convolution fusion | flops 54474368 | bytes 4856576 | tf_op jit(solution)/shard_map/dot_general | solution.py:10
  12.1 0.0 copy-done.7
  12.1 0.0 copy-done.3
  12.1 0.0 copy-done.6
  12.1 0.0 copy-done.2
  12.1 0.9 multiply_reduce_fusion
  13.0 25.5 %all-reduce = (f32[2432]{0:T(1024)S(1)}, f32[2432]{0:T(1024)S(1)}) all-reduce(f32[2432]{0:T(1024)S(1)} %get-tuple-element.6, f32[2432]{0:T(1024)S(1)} %get-tuple-element.8), channel_id=1, replica_groups=mesh['shard'=8,'tp'=4] {'shard'}, use_global_device_ids=true, to_apply=%region_1.0 | all-reduce | flops 4864 | bytes 38912 | tf_op jit(solution)/shard_map/psum | solution.py:18
  38.5 0.0 copy-start.4
  38.6 3.2 %divide_convert_fusion.1 = bf16[320,2432]{1,0:T(8,128)(2,1)} fusion(f32[320,2432]{1,0:T(8,128)} %get-tuple-element.7, f32[2432]{0:T(1024)S(1)} %sqrt.6), kind=kLoop, calls=%fused_computation.8 | loop fusion | flops 1556480 | bytes 4679168 | tf_op jit(solution)/shard_map/convert_element_type | solution.py:28
  41.8 0.0 all-gather.3.cloned.1.call-update
  41.8 0.0 copy-done.4
  41.8 0.0 all-gather.5.cloned.1.call-start
  41.9 0.0 copy-start.5
  41.9 1.3 divide_convert_fusion
  43.2 0.0 all-gather.5.cloned.1.call-update
  43.2 0.0 copy-done.5
  43.2 69.5 %all-gather.3.cloned.1.call-done = bf16[2560,2432]{1,0:T(8,128)(2,1)} async-done(((bf16[320,2432]{1,0:T(8,128)(2,1)}), bf16[2560,2432]{1,0:T(8,128)(2,1)}) %all-gather.3.cloned.1.call-update) | async-done | bytes 12451856 | tf_op jit(solution)/shard_map/all_gather | solution.py:32
  112.8 73.9 %all-gather.5.cloned.1.call-done = bf16[2560,2432]{1,0:T(8,128)(2,1)} async-done(((bf16[320,2432]{1,0:T(8,128)(2,1)}), bf16[2560,2432]{1,0:T(8,128)(2,1)}) %all-gather.5.cloned.1.call-update) | async-done | bytes 12451856 | tf_op jit(solution)/shard_map/all_gather | solution.py:33
  186.7 0.0 copy-start.1
  186.7 11.0 %copy.13 = bf16[2560,2432]{1,0:T(8,128)(2,1)} copy(bf16[2560,2432]{1,0:T(8,128)(2,1)} %all-gather.3.cloned.1.call-done) | data formatting | bytes 24903680
  197.7 1.8 copy-done.1
  199.5 4.7 %copy.14 = bf16[2560,2432]{1,0:T(8,128)(2,1)} copy(bf16[2560,2432]{1,0:T(8,128)(2,1)S(1)} %copy-done.1) | data formatting | bytes 24903680
  (2 shorter events, 0.0 us)
Async XLA Ops:
  7.2 0.9 copy-start
  7.2 4.9 %copy-start.7 = (f32[320]{0:T(512)S(1)}, f32[320]{0:T(512)}, u32[]{:S(2)}) copy-start(f32[320]{0:T(512)} %param.13) | copy-start | bytes 3844
  7.2 4.9 %copy-start.3 = (bf16[32,2432]{1,0:T(8,128)(2,1)S(1)}, bf16[32,2432]{1,0:T(8,128)(2,1)}, u32[]{:S(2)}) copy-start(bf16[32,2432]{1,0:T(8,128)(2,1)} %param.12) | copy-start | bytes 466948
  7.2 4.9 %copy-start.6 = (bf16[320,32]{0,1:T(8,128)(2,1)S(1)}, bf16[320,32]{0,1:T(8,128)(2,1)}, u32[]{:S(2)}) copy-start(bf16[320,32]{0,1:T(8,128)(2,1)} %param.11) | copy-start | bytes 61444
  7.2 105.5 %all-gather.3.cloned.1.call-start = ((), (), s32[]{:S(2)}) async-start(), calls=%async_computation | async-start | bytes 14008320 | tf_op jit(solution)/shard_map/all_gather | solution.py:32
  8.1 4.0 %copy-start.2 = (bf16[320,2432]{1,0:T(8,128)(2,1)S(1)}, bf16[320,2432]{1,0:T(8,128)(2,1)}, u32[]{:S(2)}) copy-start(bf16[320,2432]{1,0:T(8,128)(2,1)} %param.10) | copy-start | bytes 4669444
  38.5 3.3 %copy-start.4 = (f32[2432]{0:T(1024)}, f32[2432]{0:T(1024)S(1)}, u32[]{:S(2)}) copy-start(f32[2432]{0:T(1024)S(1)} %sqrt.6) | copy-start | bytes 29188
  41.8 144.9 %all-gather.5.cloned.1.call-start = ((), (), s32[]{:S(2)}) async-start(), calls=%async_computation.1 | async-start | bytes 14008320 | tf_op jit(solution)/shard_map/all_gather | solution.py:33
  41.9 1.4 copy-start.5
  186.7 12.8 %copy-start.1 = (bf16[2560,2432]{1,0:T(8,128)(2,1)S(1)}, bf16[2560,2432]{1,0:T(8,128)(2,1)}, u32[]{:S(2)}) copy-start(bf16[2560,2432]{1,0:T(8,128)(2,1)} %all-gather.5.cloned.1.call-done) | copy-start | bytes 37355524
Sparse Core Ops, SparseCore 0:
  41.9 70.7 all-gather.2
  115.2 71.4 all-gather.4
where the time goes:
time: 211 us
  waiting for transfers between devices  143 us (68%)
  blocking collectives  25.5 us (12%)
  local copies, waits for them, and re-layouts  18.4 us (9%)
  between operations  14.1 us (7%)
  matrix products  4.88 us (2%)
  other arithmetic  4.54 us (2%)
    all_gather x1, waiting for transfers between devices, local(): lax.all_gather(narrow_up, 'shard', axis=0, tiled=True)  73.9 us
    all_gather x1, waiting for transfers between devices, local(): lax.all_gather(narrow_gate, 'shard', axis=0, tiled=True)  69.5 us
    psum x1, blocking collectives, local(): lax.psum((jnp.sum(latest_gained_gate * latest_gained_gate, axis=0), jnp.s...  25.5 us
    unnamed x18, local copies, waits for them, and re-layouts  18.4 us
  transfers between devices with their start and end apart: 2, of which 2 were waited for; matrix products, arithmetic and copies ran while one was open for 1% of the time, Pallas kernels for 0%

commit v1 on v0

v1 whole, which is shorter than its diff:
```python
import functools
import math

import jax
import jax.numpy as jnp
from jax import lax
from jax.experimental import pallas as pl
from jax.experimental.pallas import tpu as pltpu
from jax.sharding import PartitionSpec as P

mix_rate = 2.0
AXIS = "shard"


def local(weight_gate, low_gate, high_gate, weight_up, low_up, high_up, norm_gain):
    latest_gate = weight_gate.astype(jnp.float32) + mix_rate * jnp.dot(
        low_gate, high_gate, preferred_element_type=jnp.float32
    )
    latest_up = weight_up.astype(jnp.float32) + mix_rate * jnp.dot(
        low_up, high_up, preferred_element_type=jnp.float32
    )
    latest_gained_gate = latest_gate * norm_gain[:, None]
    latest_gained_up = latest_up * norm_gain[:, None]
    total_gate, total_up = lax.psum(
        (
            jnp.sum(latest_gained_gate * latest_gained_gate, axis=0),
            jnp.sum(latest_gained_up * latest_gained_up, axis=0),
        ),
        AXIS,
    )
    factor_gate = jnp.sqrt(total_gate)
    factor_up = jnp.sqrt(total_up)
    narrow_gate = (latest_gained_gate / factor_gate).astype(jnp.bfloat16)
    narrow_up = (latest_gained_up / factor_up).astype(jnp.bfloat16)
    ready_gate = lax.all_gather(narrow_gate, AXIS, axis=0, tiled=True)
    ready_up = lax.all_gather(narrow_up, AXIS, axis=0, tiled=True)
    return (ready_gate, ready_up, factor_gate, factor_up)


def gather_kernel(
    n, chunks, wg_hbm, wu_hbm, lg, lu, hg, hu, gain,
    out_g, out_u, fac,
    w_v, g_v, col_v, sums, rf_v, w_sem, ssum, rsum, send, recv,
):
    rows, cols = wg_hbm.shape
    step = rows // chunks
    me = lax.axis_index(AXIS)
    core = lax.rem(me, 2)
    x = lax.rem(me // 2, 2)
    y = me // 4
    sib = me + 1 - 2 * core
    to_x = me + 2 - 4 * x
    to_y = me + 4 - 8 * y
    diag = to_x + 4 - 8 * y

    barrier = pltpu.get_barrier_semaphore()
    for d in range(1, n):
        pl.semaphore_signal(barrier, inc=1, device_id={AXIS: lax.rem(me + d, n)})

    loads = [
        pltpu.make_async_copy(w, w_v.at[a], w_sem.at[a])
        for a, w in enumerate((wg_hbm, wu_hbm))
    ]
    for c in loads:
        c.start()

    wide = jnp.broadcast_to(gain[...], (128, gain.shape[1]))
    col_v[...] = wide.T
    lows, highs, outs = (lg, lu), (hg, hu), (out_g, out_u)
    for a in range(2):
        loads[a].wait()
        acc = jnp.zeros((8, cols), jnp.float32)
        for k in range(chunks):
            r = pl.ds(k * step, step)
            prod = jnp.dot(lows[a][r, :], highs[a][...], preferred_element_type=jnp.float32)
            new = w_v[a, r, :].astype(jnp.float32) + mix_rate * prod
            new = new * col_v[r, 0:1]
            g_v[a, r, :] = new
            acc = acc + jnp.sum((new * new).reshape(step // 8, 8, cols), axis=0)
        sums[me, :, a * cols:(a + 1) * cols] = jnp.sum(acc, axis=0, keepdims=True)

    pl.semaphore_wait(barrier, n - 1)
    shares = []
    for d in range(1, n):
        shares.append(pltpu.make_async_remote_copy(
            src_ref=sums.at[me], dst_ref=sums.at[me],
            send_sem=ssum.at[d], recv_sem=rsum.at[d],
            device_id={AXIS: lax.rem(me + d, n)}))
        shares[-1].start()
    for c in shares:
        c.wait_recv()
    total = sums[0]
    for d in range(1, n):
        total = total + sums[d]
    factor = jnp.sqrt(total)
    fac[...] = factor
    rf_v[...] = 1.0 / factor

    def move(slot, a, k, owner, target):
        r = pl.ds(pl.multiple_of(owner * rows + k * step, 16), step)
        part = outs[a].at[r, :]
        return pltpu.make_async_remote_copy(
            src_ref=part, dst_ref=part,
            send_sem=send.at[slot, a * chunks + k], recv_sem=recv.at[slot, a * chunks + k],
            device_id={AXIS: target})

    started = []

    def go(*args):
        c = move(*args)
        c.start()
        started.append(c)

    every = [(a, k) for a in range(2) for k in range(chunks)]

    def send_own(a, k):
        go(0, a, k, me, to_x)
        go(1, a, k, me, to_y)
        go(2, a, k, me, sib)

    for i, (a, k) in enumerate(every):
        new = g_v[a, k * step:(k + 1) * step, :] * rf_v[:, a * cols:(a + 1) * cols]
        r = pl.ds(pl.multiple_of(me * rows + k * step, 16), step)
        outs[a][r, :] = new.astype(jnp.bfloat16)
        if i:
            send_own(*every[i - 1])
    send_own(*every[-1])

    for a, k in every:
        move(0, a, k, to_x, to_x).wait_recv()
        if k % 2 == 0:
            go(5, a, k, to_x, to_y)
        go(3, a, k, to_x, sib)
        move(1, a, k, to_y, to_y).wait_recv()
        if k % 2 == 1:
            go(5, a, k, to_y, to_x)
        go(4, a, k, to_y, sib)
    for a, k in every:
        move(5, a, k, diag, to_x).wait_recv()
        go(6, a, k, diag, sib)
    flip = 1 - 2 * core
    for a, k in every:
        move(2, a, k, sib, sib).wait_recv()
        move(3, a, k, to_x + flip, sib).wait_recv()
        move(4, a, k, to_y + flip, sib).wait_recv()
        move(6, a, k, diag + flip, sib).wait_recv()
    for c in started:
        c.wait_send()
    for c in shares:
        c.wait_send()


def write_kernel(parts, a_v, b_v, a_hbm, b_hbm, sem):
    step = a_v.shape[0] // parts
    copies = []
    for i, (src, dst) in enumerate(((a_v, a_hbm), (b_v, b_hbm))):
        for k in range(parts):
            r = pl.ds(k * step, step)
            copies.append(pltpu.make_async_copy(src.at[r, :], dst.at[r, :], sem.at[i, k]))
    for c in copies:
        c.start()
    for c in copies:
        c.wait()


def paired(n, weight_gate, low_gate, high_gate, weight_up, low_up, high_up, norm_gain):
    rows, cols = weight_gate.shape
    chunks = 4
    full = (n * rows, cols)
    vmem = pl.BlockSpec(memory_space=pltpu.VMEM)
    hbm = pl.BlockSpec(memory_space=pl.ANY)
    padded = -(-rows // 128) * 128
    gain = jnp.pad(norm_gain, (0, padded - rows)).reshape(1, padded)
    gate, up, fac = pl.pallas_call(
        functools.partial(gather_kernel, n, chunks),
        out_shape=(
            pltpu.VMEM(full, jnp.bfloat16),
            pltpu.VMEM(full, jnp.bfloat16),
            jax.ShapeDtypeStruct((1, 2 * cols), jnp.float32),
        ),
        in_specs=[hbm, hbm] + [vmem] * 5,
        out_specs=(vmem, vmem, vmem),
        scratch_shapes=[
            pltpu.VMEM((2, rows, cols), jnp.bfloat16),
            pltpu.VMEM((2, rows, cols), jnp.float32),
            pltpu.VMEM((padded, 128), jnp.float32),
            pltpu.VMEM((n, 1, 2 * cols), jnp.float32),
            pltpu.VMEM((1, 2 * cols), jnp.float32),
            pltpu.SemaphoreType.DMA((2,)),
            pltpu.SemaphoreType.DMA((n,)),
            pltpu.SemaphoreType.DMA((n,)),
            pltpu.SemaphoreType.DMA((7, 2 * chunks)),
            pltpu.SemaphoreType.DMA((7, 2 * chunks)),
        ],
        compiler_params=pltpu.CompilerParams(
            collective_id=0, has_side_effects=True, vmem_limit_bytes=24 * 2**20
        ),
        name="merge_gather",
    )(weight_gate, weight_up, low_gate, low_up, high_gate, high_up, gain)
    parts = 8
    ready_gate, ready_up = pl.pallas_call(
        functools.partial(write_kernel, parts),
        out_shape=(jax.ShapeDtypeStruct(full, jnp.bfloat16),) * 2,
        in_specs=[vmem, vmem],
        out_specs=(hbm, hbm),
        scratch_shapes=[pltpu.SemaphoreType.DMA((2, parts))],
        compiler_params=pltpu.CompilerParams(vmem_limit_bytes=2**20),
        name="write_out",
    )(gate, up)
    return ready_gate, ready_up, fac[0, :cols], fac[0, cols:]


def solution(mesh):
    in_specs = (
        P("shard", "tp"),
        P("shard", None),
        P(None, "tp"),
        P("shard", "tp"),
        P("shard", None),
        P(None, "tp"),
        P("shard"),
    )
    out_specs = (P(None, "tp"), P(None, "tp"), P("tp"), P("tp"))
    n = mesh.shape[AXIS]
    side = math.isqrt(n // 2)
    body = functools.partial(paired, n) if side == 2 and 2 * side * side == n else local
    return jax.shard_map(body, mesh=mesh, in_specs=in_specs, out_specs=out_specs, check_vma=False)
```

time: 211 us -> 131 us (0.62)
  waiting for transfers between devices: 143 us -> 0 us
  Pallas kernels: 0 us -> 122 us
  blocking collectives: 25.5 us -> 0 us
  between operations: 14.1 us -> 0.66 us
  local copies, waits for them, and re-layouts: 18.4 us -> 7.68 us
  matrix products: 4.88 us -> 0 us
  other arithmetic: 4.54 us -> 0 us
    all_gather x2 -> x0, waiting for transfers between devices: 143 us -> none  [the longest x1 73.9 us: local(): lax.all_gather(narrow_up, 'shard', axis=0, tiled=True)]
    pallas_call x0 -> x2, Pallas kernels: none -> 122 us  [the longest x1 113 us: paired(): pl.pallas_call(functools.partial(gather_kernel, n, chunks), out_shape=(pl...]
    psum x1 -> x0, blocking collectives: 25.5 us -> none  [local(): lax.psum((jnp.sum(latest_gained_gate * latest_gained_gate, axis=0), jnp.s...]
    unnamed x18 -> x10, local copies, waits for them, and re-layouts: 18.4 us -> 6.34 us
    dot_general x2 -> x0, matrix products: 4.88 us -> none  [the longest x1 4.01 us: local(): jnp.dot(low_gate, high_gate, preferred_element_type=jnp.float32)]
    convert_element_type x2 -> x0, other arithmetic: 4.54 us -> none  [the longest x1 3.21 us: local(): (latest_gained_gate / factor_gate).astype(jnp.bfloat16)]
  transfers between devices with their start and end apart: 2 -> 0, of which waited for: 2 -> 0; matrix products, arithmetic and copies ran while one was open for 1% -> 0% of each run, Pallas kernels for 0% -> 0%
where the time goes in v1:
time: 131 us; the launch traced here: 130 us
  Pallas kernels  122 us (93%)
  local copies, waits for them, and re-layouts  7.68 us (6%)
    pallas_call x1, Pallas kernels, paired(): pl.pallas_call(functools.partial(gather_kernel, n, chunks), out_shape=(pl...  113 us
    pallas_call x1, Pallas kernels, paired(): pl.pallas_call(functools.partial(write_kernel, parts), out_shape=(jax.Sha...  8.43 us
    unnamed x10, local copies, waits for them, and re-layouts  6.34 us

profile of v1, /device:TPU:0, one launch (start us, length us, event | category | flops | bytes accessed | tf_op | source)
XLA Modules:
  0.0 130.2 jit_solution(3400109231526662239)
XLA Ops:
  0.6 0.7 pad.4
  1.3 0.9 copy.11.lg
  2.2 0.9 copy.12.lu
  3.0 0.0 copy-start
  3.0 1.4 %copy-done = bf16[320,2432]{1,0:T(8,128)(2,1)S(1)} copy-done((bf16[320,2432]{1,0:T(8,128)(2,1)S(1)}, bf16[320,2432]{1,0:T(8,128)(2,1)}, u32[]{:S(2)}) %copy-start) | copy-done | bytes 1556504
  4.4 0.0 copy-start.1
  4.4 1.4 %copy-done.1 = bf16[320,2432]{1,0:T(8,128)(2,1)S(1)} copy-done((bf16[320,2432]{1,0:T(8,128)(2,1)S(1)}, bf16[320,2432]{1,0:T(8,128)(2,1)}, u32[]{:S(2)}) %copy-start.1) | copy-done | bytes 1556504
  5.8 0.0 copy-start.2
  5.8 0.9 copy-done.2
  6.8 0.0 copy-start.3
  6.8 0.9 copy-done.3
  7.7 113.5 %merge_gather.1 = (bf16[2560,2432]{1,0:T(8,128)(2,1)S(1)}, bf16[2560,2432]{1,0:T(8,128)(2,1)S(1)}, f32[1,4864]{1,0:T(1,128)S(1)}) custom-call(bf16[320,2432]{1,0:T(8,128)(2,1)S(1)} %copy-done, bf16[320,2432]{1,0:T(8,128)(2,1)S(1)} %copy-done.1, bf16[320,32]{1,0:T(8,128)(2,1)S(1)} %copy.11.lg, bf16[320,32]{1,0:T(8,128)(2,1)S(1)} %copy.12.lu, ...), custom_call_target="tpu_custom_call" | custom-call | tf_op jit(solution)/shard_map/merge_gather/pallas_call | solution.py:174
  121.1 8.4 %write_out.1 = (bf16[2560,2432]{1,0:T(8,128)(2,1)}, bf16[2560,2432]{1,0:T(8,128)(2,1)}) custom-call(bf16[2560,2432]{1,0:T(8,128)(2,1)S(1)} %get-tuple-element.9.a_v, bf16[2560,2432]{1,0:T(8,128)(2,1)S(1)} %get-tuple-element.10.b_v), custom_call_target="tpu_custom_call" | custom-call | tf_op jit(solution)/shard_map/write_out/pallas_call | solution.py:201
  129.6 0.6 slice_reduce_fusion
  (1 shorter events, 0.0 us)
Async XLA Ops:
  3.0 1.4 %copy-start = (bf16[320,2432]{1,0:T(8,128)(2,1)S(1)}, bf16[320,2432]{1,0:T(8,128)(2,1)}, u32[]{:S(2)}) copy-start(bf16[320,2432]{1,0:T(8,128)(2,1)} %wg_hbm.1) | copy-start | bytes 4669444
  4.4 1.4 %copy-start.1 = (bf16[320,2432]{1,0:T(8,128)(2,1)S(1)}, bf16[320,2432]{1,0:T(8,128)(2,1)}, u32[]{:S(2)}) copy-start(bf16[320,2432]{1,0:T(8,128)(2,1)} %wu_hbm.1) | copy-start | bytes 4669444
  5.8 0.9 copy-start.2
  6.8 0.9 copy-start.3

commit v2 on v1

--- a/solution.py
+++ b/solution.py
@@ -38,9 +38,10 @@
 
 
 def gather_kernel(
-    n, chunks, wg_hbm, wu_hbm, lg, lu, hg, hu, gain,
+    n, chunks, wg_hbm, wu_hbm, lg_hbm, lu_hbm, hg_hbm, hu_hbm, gain_hbm,
     out_g, out_u, fac,
-    w_v, g_v, col_v, sums, rf_v, w_sem, ssum, rsum, send, recv,
+    w_v, l_v, h_v, gain_v, low_v, g_v, col_v, sums, rf_v,
+    in_sem, ssum, rsum, send, recv,
 ):
     rows, cols = wg_hbm.shape
     step = rows // chunks
@@ -57,24 +58,34 @@
     for d in range(1, n):
         pl.semaphore_signal(barrier, inc=1, device_id={AXIS: lax.rem(me + d, n)})
 
-    loads = [
-        pltpu.make_async_copy(w, w_v.at[a], w_sem.at[a])
-        for a, w in enumerate((wg_hbm, wu_hbm))
-    ]
-    for c in loads:
-        c.start()
-
-    wide = jnp.broadcast_to(gain[...], (128, gain.shape[1]))
-    col_v[...] = wide.T
-    lows, highs, outs = (lg, lu), (hg, hu), (out_g, out_u)
+    gain_load = pltpu.make_async_copy(gain_hbm, gain_v, in_sem.at[6])
+    low_loads, high_loads, loads = (
+        [
+            pltpu.make_async_copy(src, dst.at[a], in_sem.at[3 * a + i])
+            for a, src in enumerate(pair)
+        ]
+        for i, (pair, dst) in enumerate((
+            ((lg_hbm, lu_hbm), l_v), ((hg_hbm, hu_hbm), h_v), ((wg_hbm, wu_hbm), w_v)
+        ))
+    )
+    gain_load.start()
     for a in range(2):
+        for c in (low_loads[a], high_loads[a], loads[a]):
+            c.start()
+
+    gain_load.wait()
+    col_v[...] = jnp.broadcast_to(gain_v[...], (128, rows)).T
+    outs = (out_g, out_u)
+    for a in range(2):
+        low_loads[a].wait()
+        low_v[a] = (mix_rate * l_v[a].astype(jnp.float32)).T.astype(jnp.bfloat16)
+        high_loads[a].wait()
         loads[a].wait()
         acc = jnp.zeros((8, cols), jnp.float32)
         for k in range(chunks):
             r = pl.ds(k * step, step)
-            prod = jnp.dot(lows[a][r, :], highs[a][...], preferred_element_type=jnp.float32)
-            new = w_v[a, r, :].astype(jnp.float32) + mix_rate * prod
-            new = new * col_v[r, 0:1]
+            prod = jnp.dot(low_v[a, r, :], h_v[a], preferred_element_type=jnp.float32)
+            new = (w_v[a, r, :].astype(jnp.float32) + prod) * col_v[r, 0:1]
             g_v[a, r, :] = new
             acc = acc + jnp.sum((new * new).reshape(step // 8, 8, cols), axis=0)
         sums[me, :, a * cols:(a + 1) * cols] = jnp.sum(acc, axis=0, keepdims=True)
@@ -169,8 +180,10 @@
     full = (n * rows, cols)
     vmem = pl.BlockSpec(memory_space=pltpu.VMEM)
     hbm = pl.BlockSpec(memory_space=pl.ANY)
-    padded = -(-rows // 128) * 128
-    gain = jnp.pad(norm_gain, (0, padded - rows)).reshape(1, padded)
+    gain = norm_gain.reshape(1, rows)
+    space = pl.BlockSpec(memory_space=pltpu.HBM)
+    rank = high_gate.shape[0]
+    grant = 65472 * 2**10 - (4 * full[0] * cols + 8 * cols) // 2**10 * 2**10 - 24 * 2**10
     gate, up, fac = pl.pallas_call(
         functools.partial(gather_kernel, n, chunks),
         out_shape=(
@@ -178,25 +191,29 @@
             pltpu.VMEM(full, jnp.bfloat16),
             jax.ShapeDtypeStruct((1, 2 * cols), jnp.float32),
         ),
-        in_specs=[hbm, hbm] + [vmem] * 5,
+        in_specs=[space] * 7,
         out_specs=(vmem, vmem, vmem),
         scratch_shapes=[
             pltpu.VMEM((2, rows, cols), jnp.bfloat16),
+            pltpu.VMEM((2, rank, rows), jnp.bfloat16),
+            pltpu.VMEM((2, rank, cols), jnp.bfloat16),
+            pltpu.VMEM((1, rows), jnp.float32),
+            pltpu.VMEM((2, rows, rank), jnp.bfloat16),
             pltpu.VMEM((2, rows, cols), jnp.float32),
-            pltpu.VMEM((padded, 128), jnp.float32),
+            pltpu.VMEM((rows, 128), jnp.float32),
             pltpu.VMEM((n, 1, 2 * cols), jnp.float32),
             pltpu.VMEM((1, 2 * cols), jnp.float32),
-            pltpu.SemaphoreType.DMA((2,)),
+            pltpu.SemaphoreType.DMA((7,)),
             pltpu.SemaphoreType.DMA((n,)),
             pltpu.SemaphoreType.DMA((n,)),
             pltpu.SemaphoreType.DMA((7, 2 * chunks)),
             pltpu.SemaphoreType.DMA((7, 2 * chunks)),
         ],
         compiler_params=pltpu.CompilerParams(
-            collective_id=0, has_side_effects=True, vmem_limit_bytes=24 * 2**20
+            collective_id=0, has_side_effects=True, vmem_limit_bytes=grant
         ),
         name="merge_gather",
-    )(weight_gate, weight_up, low_gate, low_up, high_gate, high_up, gain)
+    )(weight_gate, weight_up, low_gate.T, low_up.T, high_gate, high_up, gain)
     parts = 8
     ready_gate, ready_up = pl.pallas_call(
         functools.partial(write_kernel, parts),

time: 131 us -> 126 us (0.962)
  local copies, waits for them, and re-layouts: 7.68 us -> 1.9 us
    unnamed x10 -> x2, local copies, waits for them, and re-layouts: 6.34 us -> 0.01 us
where the time goes in v2:
time: 126 us
  Pallas kernels  123 us (98%)
  local copies, waits for them, and re-layouts  1.9 us (2%)
    pallas_call x1, Pallas kernels, paired(): pl.pallas_call(functools.partial(gather_kernel, n, chunks), out_shape=(pl...  115 us
    pallas_call x1, Pallas kernels, paired(): pl.pallas_call(functools.partial(write_kernel, parts), out_shape=(jax.Sha...  8.43 us

profile of v2, /device:TPU:0, one launch (start us, length us, event | category | flops | bytes accessed | tf_op | source)
XLA Modules:
  0.0 125.6 jit_solution(8393002575374195374)
XLA Ops:
  0.6 1.2 reshape.11.gain_hbm
  1.9 114.6 %merge_gather.1 = (bf16[2560,2432]{1,0:T(8,128)(2,1)S(1)}, bf16[2560,2432]{1,0:T(8,128)(2,1)S(1)}, f32[1,4864]{1,0:T(1,128)}) custom-call(bf16[320,2432]{1,0:T(8,128)(2,1)} %wg_hbm.1, bf16[320,2432]{1,0:T(8,128)(2,1)} %wu_hbm.1, bf16[32,320]{1,0:T(8,128)(2,1)} %bitcast.2, bf16[32,320]{1,0:T(8,128)(2,1)} %bitcast.3, bf16[32,2432]{1,0:T(8,128)(2,1)} %hg_hbm.1, ...), custom_call_target="tpu_custom_call" | custom-call | tf_op jit(solution)/shard_map/merge_gather/pallas_call | solution.py:187
  116.5 0.0 copy-start
  116.5 8.4 %write_out.1 = (bf16[2560,2432]{1,0:T(8,128)(2,1)}, bf16[2560,2432]{1,0:T(8,128)(2,1)}) custom-call(bf16[2560,2432]{1,0:T(8,128)(2,1)S(1)} %get-tuple-element.9.a_v, bf16[2560,2432]{1,0:T(8,128)(2,1)S(1)} %get-tuple-element.10.b_v), custom_call_target="tpu_custom_call" | custom-call | tf_op jit(solution)/shard_map/write_out/pallas_call | solution.py:218
  125.0 0.0 copy-done
  125.0 0.6 slice_reduce_fusion
Async XLA Ops:
  116.5 8.5 %copy-start = (f32[1,4864]{1,0:T(1,128)S(1)}, f32[1,4864]{1,0:T(1,128)}, u32[]{:S(2)}) copy-start(f32[1,4864]{1,0:T(1,128)} %get-tuple-element.13) | copy-start | bytes 58372

commit v3 on v2

--- a/solution.py
+++ b/solution.py
@@ -38,10 +38,10 @@
 
 
 def gather_kernel(
-    n, chunks, wg_hbm, wu_hbm, lg_hbm, lu_hbm, hg_hbm, hu_hbm, gain_hbm,
+    n, chunks, raw, wg_hbm, wu_hbm, lg_hbm, lu_hbm, hg_hbm, hu_hbm, gain_hbm,
     out_g, out_u, fac,
-    w_v, l_v, h_v, gain_v, low_v, g_v, col_v, sums, rf_v,
-    in_sem, ssum, rsum, send, recv,
+    w_v, l_v, h_v, gain_v, low_v, g_v, col_v, sums, rf_v, far_low,
+    in_sem, ssum, rsum, slow, rlow, send, recv,
 ):
     rows, cols = wg_hbm.shape
     step = rows // chunks
@@ -73,9 +73,39 @@
         for c in (low_loads[a], high_loads[a], loads[a]):
             c.start()
 
+    early = raw * step
+    outs = (out_g, out_u)
+    every = [(a, k) for a in range(2) for k in range(chunks)]
+    started = {}
+
+    def move(slot, a, k, owner, target, base=None):
+        r = pl.ds(pl.multiple_of(owner * rows + k * step, 16), step)
+        part = outs[a].at[r, :]
+        return pltpu.make_async_remote_copy(
+            src_ref=part if base is None else base.at[k * step:(k + 1) * step, :],
+            dst_ref=part,
+            send_sem=send.at[slot, a * chunks + k], recv_sem=recv.at[slot, a * chunks + k],
+            device_id={AXIS: target})
+
+    def go(*args):
+        started[args[:3]] = move(*args)
+        started[args[:3]].start()
+
+    def send_own(a, k):
+        go(0, a, k, me, to_x)
+        go(1, a, k, me, to_y)
+        go(2, a, k, me, sib)
+
+    def send_raw(a, k):
+        go(0, a, k, me, to_x, wg_hbm)
+        go(1, a, k, me, to_y, wg_hbm)
+        go(2, a, k, me, sib, wg_hbm)
+
+    pl.semaphore_wait(barrier, n - 1)
+    send_raw(0, 0)
+
     gain_load.wait()
     col_v[...] = jnp.broadcast_to(gain_v[...], (128, rows)).T
-    outs = (out_g, out_u)
     for a in range(2):
         low_loads[a].wait()
         low_v[a] = (mix_rate * l_v[a].astype(jnp.float32)).T.astype(jnp.bfloat16)
@@ -90,7 +120,7 @@
             acc = acc + jnp.sum((new * new).reshape(step // 8, 8, cols), axis=0)
         sums[me, :, a * cols:(a + 1) * cols] = jnp.sum(acc, axis=0, keepdims=True)
 
-    pl.semaphore_wait(barrier, n - 1)
+    sums[me, :, 2 * cols:] = gain_v[:, :early]
     shares = []
     for d in range(1, n):
         shares.append(pltpu.make_async_remote_copy(
@@ -98,66 +128,78 @@
             send_sem=ssum.at[d], recv_sem=rsum.at[d],
             device_id={AXIS: lax.rem(me + d, n)}))
         shares[-1].start()
+    lows = []
+    for d in range(1, n):
+        lows.append(pltpu.make_async_remote_copy(
+            src_ref=l_v.at[0, :, :early], dst_ref=far_low.at[me],
+            send_sem=slow.at[d], recv_sem=rlow.at[d],
+            device_id={AXIS: lax.rem(me + d, n)}))
+        lows[-1].start()
+    for k in range(1, raw):
+        send_raw(0, k)
     for c in shares:
         c.wait_recv()
-    total = sums[0]
-    for d in range(1, n):
-        total = total + sums[d]
+    total = sums[0, :, :2 * cols]
+    for d in range(1, n):
+        total = total + sums[d, :, :2 * cols]
     factor = jnp.sqrt(total)
     fac[...] = factor
     rf_v[...] = 1.0 / factor
-
-    def move(slot, a, k, owner, target):
-        r = pl.ds(pl.multiple_of(owner * rows + k * step, 16), step)
-        part = outs[a].at[r, :]
-        return pltpu.make_async_remote_copy(
-            src_ref=part, dst_ref=part,
-            send_sem=send.at[slot, a * chunks + k], recv_sem=recv.at[slot, a * chunks + k],
-            device_id={AXIS: target})
-
-    started = []
-
-    def go(*args):
-        c = move(*args)
-        c.start()
-        started.append(c)
-
-    every = [(a, k) for a in range(2) for k in range(chunks)]
-
-    def send_own(a, k):
-        go(0, a, k, me, to_x)
-        go(1, a, k, me, to_y)
-        go(2, a, k, me, sib)
 
     for i, (a, k) in enumerate(every):
         new = g_v[a, k * step:(k + 1) * step, :] * rf_v[:, a * cols:(a + 1) * cols]
         r = pl.ds(pl.multiple_of(me * rows + k * step, 16), step)
         outs[a][r, :] = new.astype(jnp.bfloat16)
-        if i:
+        if i > raw:
             send_own(*every[i - 1])
     send_own(*every[-1])
 
-    for a, k in every:
+    for i, (a, k) in enumerate(every):
         move(0, a, k, to_x, to_x).wait_recv()
-        if k % 2 == 0:
+        if i % 2 == 0:
             go(5, a, k, to_x, to_y)
         go(3, a, k, to_x, sib)
         move(1, a, k, to_y, to_y).wait_recv()
-        if k % 2 == 1:
+        if i % 2 == 1:
             go(5, a, k, to_y, to_x)
         go(4, a, k, to_y, sib)
-    for a, k in every:
-        move(5, a, k, diag, to_x).wait_recv()
-        go(6, a, k, diag, sib)
+
     flip = 1 - 2 * core
-    for a, k in every:
+
+    def from_sib(a, k):
         move(2, a, k, sib, sib).wait_recv()
         move(3, a, k, to_x + flip, sib).wait_recv()
         move(4, a, k, to_y + flip, sib).wait_recv()
         move(6, a, k, diag + flip, sib).wait_recv()
-    for c in started:
+
+    def finish_raw():
+        for a, k in every[:raw]:
+            from_sib(a, k)
+            for slot in (3, 4, 5, 6):
+                started.pop((slot, a, k)).wait_send()
+        for c in lows:
+            c.wait_recv()
+
+        @pl.loop(1, n)
+        def _(d):
+            owner = lax.rem(me + d, n)
+            low = (mix_rate * far_low[owner].astype(jnp.float32)).T.astype(jnp.bfloat16)
+            col = jnp.broadcast_to(sums[owner, :, 2 * cols:], (128, early)).T[:, 0:1]
+            r = pl.ds(pl.multiple_of(owner * rows, 16), early)
+            prod = jnp.dot(low, h_v[0], preferred_element_type=jnp.float32)
+            new = (out_g[r, :].astype(jnp.float32) + prod) * col
+            out_g[r, :] = (new * rf_v[:, :cols]).astype(jnp.bfloat16)
+
+    for i, (a, k) in enumerate(every):
+        if i == 3 * raw:
+            finish_raw()
+        move(5, a, k, diag, to_x).wait_recv()
+        go(6, a, k, diag, sib)
+    for a, k in every[raw:]:
+        from_sib(a, k)
+    for c in started.values():
         c.wait_send()
-    for c in shares:
+    for c in shares + lows:
         c.wait_send()
 
 
@@ -176,7 +218,8 @@
 
 def paired(n, weight_gate, low_gate, high_gate, weight_up, low_up, high_up, norm_gain):
     rows, cols = weight_gate.shape
-    chunks = 4
+    chunks, raw = 5, 2
+    early = raw * rows // chunks
     full = (n * rows, cols)
     vmem = pl.BlockSpec(memory_space=pltpu.VMEM)
     hbm = pl.BlockSpec(memory_space=pl.ANY)
@@ -185,7 +228,7 @@
     rank = high_gate.shape[0]
     grant = 65472 * 2**10 - (4 * full[0] * cols + 8 * cols) // 2**10 * 2**10 - 24 * 2**10
     gate, up, fac = pl.pallas_call(
-        functools.partial(gather_kernel, n, chunks),
+        functools.partial(gather_kernel, n, chunks, raw),
         out_shape=(
             pltpu.VMEM(full, jnp.bfloat16),
             pltpu.VMEM(full, jnp.bfloat16),
@@ -201,9 +244,12 @@
             pltpu.VMEM((2, rows, rank), jnp.bfloat16),
             pltpu.VMEM((2, rows, cols), jnp.float32),
             pltpu.VMEM((rows, 128), jnp.float32),
-            pltpu.VMEM((n, 1, 2 * cols), jnp.float32),
+            pltpu.VMEM((n, 1, 2 * cols + early), jnp.float32),
             pltpu.VMEM((1, 2 * cols), jnp.float32),
+            pltpu.VMEM((n, rank, early), jnp.bfloat16),
             pltpu.SemaphoreType.DMA((7,)),
+            pltpu.SemaphoreType.DMA((n,)),
+            pltpu.SemaphoreType.DMA((n,)),
             pltpu.SemaphoreType.DMA((n,)),
             pltpu.SemaphoreType.DMA((n,)),
             pltpu.SemaphoreType.DMA((7, 2 * chunks)),

time: 126 us -> 123 us (0.976)
  Pallas kernels: 123 us -> 121 us
    pallas_call x1, Pallas kernels: 115 us -> 112 us  [paired(): pl.pallas_call(functools.partial(gather_kernel, n, chunks, raw), out_shap...]
where the time goes in v3:
time: 123 us
  Pallas kernels  121 us (98%)
  local copies, waits for them, and re-layouts  1.9 us (2%)
    pallas_call x1, Pallas kernels, paired(): pl.pallas_call(functools.partial(gather_kernel, n, chunks, raw), out_shap...  112 us
    pallas_call x1, Pallas kernels, paired(): pl.pallas_call(functools.partial(write_kernel, parts), out_shape=(jax.Sha...  8.43 us

profile of v3, /device:TPU:0, one launch (start us, length us, event | category | flops | bytes accessed | tf_op | source)
XLA Modules:
  0.0 123.1 jit_solution(13026275068431772518)
XLA Ops:
  0.6 1.2 %reshape.11.gain_hbm = f32[1,320]{1,0:T(1,128)} reshape(f32[320]{0:T(512)} %param.13) | data formatting | bytes 2560 | tf_op jit(solution)/shard_map/reshape | solution.py:226
  1.9 112.1 %merge_gather.1 = (bf16[2560,2432]{1,0:T(8,128)(2,1)S(1)}, bf16[2560,2432]{1,0:T(8,128)(2,1)S(1)}, f32[1,4864]{1,0:T(1,128)}) custom-call(bf16[320,2432]{1,0:T(8,128)(2,1)} %wg_hbm.1, bf16[320,2432]{1,0:T(8,128)(2,1)} %wu_hbm.1, bf16[32,320]{1,0:T(8,128)(2,1)} %bitcast.2, bf16[32,320]{1,0:T(8,128)(2,1)} %bitcast.3, bf16[32,2432]{1,0:T(8,128)(2,1)} %hg_hbm.1, ...), custom_call_target="tpu_custom_call" | custom-call | tf_op jit(solution)/shard_map/merge_gather/pallas_call | solution.py:230
  114.0 0.0 copy-start
  114.0 8.4 %write_out.1 = (bf16[2560,2432]{1,0:T(8,128)(2,1)}, bf16[2560,2432]{1,0:T(8,128)(2,1)}) custom-call(bf16[2560,2432]{1,0:T(8,128)(2,1)S(1)} %get-tuple-element.9.a_v, bf16[2560,2432]{1,0:T(8,128)(2,1)S(1)} %get-tuple-element.10.b_v), custom_call_target="tpu_custom_call" | custom-call | tf_op jit(solution)/shard_map/write_out/pallas_call | solution.py:264
  122.4 0.0 copy-done
  122.4 0.6 slice_reduce_fusion
Async XLA Ops:
  114.0 8.5 %copy-start = (f32[1,4864]{1,0:T(1,128)S(1)}, f32[1,4864]{1,0:T(1,128)}, u32[]{:S(2)}) copy-start(f32[1,4864]{1,0:T(1,128)} %get-tuple-element.13) | copy-start | bytes 58372

commit v4 on v3

--- a/solution.py
+++ b/solution.py
@@ -105,7 +105,8 @@
     send_raw(0, 0)
 
     gain_load.wait()
-    col_v[...] = jnp.broadcast_to(gain_v[...], (128, rows)).T
+    gain = gain_v[...].reshape(1, rows)
+    col_v[...] = jnp.broadcast_to(gain, (128, rows)).T
     for a in range(2):
         low_loads[a].wait()
         low_v[a] = (mix_rate * l_v[a].astype(jnp.float32)).T.astype(jnp.bfloat16)
@@ -120,7 +121,7 @@
             acc = acc + jnp.sum((new * new).reshape(step // 8, 8, cols), axis=0)
         sums[me, :, a * cols:(a + 1) * cols] = jnp.sum(acc, axis=0, keepdims=True)
 
-    sums[me, :, 2 * cols:] = gain_v[:, :early]
+    sums[me, :, 2 * cols:] = gain[:, :early]
     shares = []
     for d in range(1, n):
         shares.append(pltpu.make_async_remote_copy(
@@ -203,8 +204,13 @@
         c.wait_send()
 
 
-def write_kernel(parts, a_v, b_v, a_hbm, b_hbm, sem):
+def write_kernel(
+    parts, a_v, b_v, fac, a_hbm, b_hbm, fa_hbm, fb_hbm, fac_v, fa_v, fb_v, sem, fsem
+):
     step = a_v.shape[0] // parts
+    cols = a_v.shape[1]
+    load = pltpu.make_async_copy(fac, fac_v, fsem.at[0])
+    load.start()
     copies = []
     for i, (src, dst) in enumerate(((a_v, a_hbm), (b_v, b_hbm))):
         for k in range(parts):
@@ -212,6 +218,11 @@
             copies.append(pltpu.make_async_copy(src.at[r, :], dst.at[r, :], sem.at[i, k]))
     for c in copies:
         c.start()
+    load.wait()
+    for i, (line, dst) in enumerate(((fa_v, fa_hbm), (fb_v, fb_hbm))):
+        line[...] = fac_v[0, i * cols:(i + 1) * cols]
+        copies.append(pltpu.make_async_copy(line, dst, fsem.at[1 + i]))
+        copies[-1].start()
     for c in copies:
         c.wait()
 
@@ -223,7 +234,7 @@
     full = (n * rows, cols)
     vmem = pl.BlockSpec(memory_space=pltpu.VMEM)
     hbm = pl.BlockSpec(memory_space=pl.ANY)
-    gain = norm_gain.reshape(1, rows)
+    gain = norm_gain
     space = pl.BlockSpec(memory_space=pltpu.HBM)
     rank = high_gate.shape[0]
     grant = 65472 * 2**10 - (4 * full[0] * cols + 8 * cols) // 2**10 * 2**10 - 24 * 2**10
@@ -240,7 +251,7 @@
             pltpu.VMEM((2, rows, cols), jnp.bfloat16),
             pltpu.VMEM((2, rank, rows), jnp.bfloat16),
             pltpu.VMEM((2, rank, cols), jnp.bfloat16),
-            pltpu.VMEM((1, rows), jnp.float32),
+            pltpu.VMEM((rows,), jnp.float32),
             pltpu.VMEM((2, rows, rank), jnp.bfloat16),
             pltpu.VMEM((2, rows, cols), jnp.float32),
             pltpu.VMEM((rows, 128), jnp.float32),
@@ -261,16 +272,22 @@
         name="merge_gather",
     )(weight_gate, weight_up, low_gate.T, low_up.T, high_gate, high_up, gain)
     parts = 8
-    ready_gate, ready_up = pl.pallas_call(
+    return tuple(pl.pallas_call(
         functools.partial(write_kernel, parts),
-        out_shape=(jax.ShapeDtypeStruct(full, jnp.bfloat16),) * 2,
-        in_specs=[vmem, vmem],
-        out_specs=(hbm, hbm),
-        scratch_shapes=[pltpu.SemaphoreType.DMA((2, parts))],
-        compiler_params=pltpu.CompilerParams(vmem_limit_bytes=2**20),
+        out_shape=(jax.ShapeDtypeStruct(full, jnp.bfloat16),) * 2
+        + (jax.ShapeDtypeStruct((cols,), jnp.float32),) * 2,
+        in_specs=[vmem, vmem, hbm],
+        out_specs=(hbm,) * 4,
+        scratch_shapes=[
+            pltpu.VMEM((1, 2 * cols), jnp.float32),
+            pltpu.VMEM((cols,), jnp.float32),
+            pltpu.VMEM((cols,), jnp.float32),
+            pltpu.SemaphoreType.DMA((2, parts)),
+            pltpu.SemaphoreType.DMA((3,)),
+        ],
+        compiler_params=pltpu.CompilerParams(vmem_limit_bytes=grant),
         name="write_out",
-    )(gate, up)
-    return ready_gate, ready_up, fac[0, :cols], fac[0, cols:]
+    )(gate, up, fac))
 
 
 def solution(mesh):

time: 123 us -> 131 us (1.065)
  Pallas kernels: 121 us -> 125 us
  local copies, waits for them, and re-layouts: 1.9 us -> 5.24 us
    unnamed x2 -> x4, local copies, waits for them, and re-layouts: 0.01 us -> 5.24 us
    pallas_call x1, Pallas kernels: 8.43 us -> 13 us  [paired(): pl.pallas_call(functools.partial(write_kernel, parts), out_shape=(jax.Sha...]
where the time goes in v4:
time: 131 us
  Pallas kernels  125 us (95%)
  local copies, waits for them, and re-layouts  5.24 us (4%)
    pallas_call x1, Pallas kernels, paired(): pl.pallas_call(functools.partial(gather_kernel, n, chunks, raw), out_shap...  112 us
    pallas_call x1, Pallas kernels, paired(): pl.pallas_call(functools.partial(write_kernel, parts), out_shape=(jax.Sha...  13 us
    unnamed x4, local copies, waits for them, and re-layouts  5.24 us

profile of v4, /device:TPU:0, one launch (start us, length us, event | category | flops | bytes accessed | tf_op | source)
XLA Modules:
  0.0 131.1 jit_solution(12337120558005019594)
XLA Ops:
  0.6 112.2 %merge_gather.1 = (bf16[2560,2432]{1,0:T(8,128)(2,1)S(1)}, bf16[2560,2432]{1,0:T(8,128)(2,1)S(1)}, f32[1,4864]{1,0:T(1,128)}) custom-call(bf16[320,2432]{1,0:T(8,128)(2,1)} %wg_hbm.1, bf16[320,2432]{1,0:T(8,128)(2,1)} %wu_hbm.1, bf16[32,320]{1,0:T(8,128)(2,1)} %bitcast.2, bf16[32,320]{1,0:T(8,128)(2,1)} %bitcast.3, bf16[32,2432]{1,0:T(8,128)(2,1)} %hg_hbm.1, ...), custom_call_target="tpu_custom_call" | custom-call | tf_op jit(solution)/shard_map/merge_gather/pallas_call | solution.py:241
  112.8 0.0 copy-start
  112.8 4.5 %copy-done = bf16[2560,2432]{1,0:T(8,128)(2,1)} copy-done((bf16[2560,2432]{1,0:T(8,128)(2,1)}, bf16[2560,2432]{1,0:T(8,128)(2,1)S(1)}, u32[]{:S(2)}) %copy-start) | copy-done | bytes 12451864
  117.3 0.0 copy-start.1
  117.3 0.7 copy-done.1
  118.1 13.0 %write_out.1 = (bf16[2560,2432]{1,0:T(8,128)(2,1)}, bf16[2560,2432]{1,0:T(8,128)(2,1)}, f32[2432]{0:T(1024)}, f32[2432]{0:T(1024)}) custom-call(bf16[2560,2432]{1,0:T(8,128)(2,1)S(1)} %get-tuple-element.7.a_v, bf16[2560,2432]{1,0:T(8,128)(2,1)} %copy-done, f32[1,4864]{1,0:T(1,128)S(1)} %copy-done.1), custom_call_target="tpu_custom_call" | custom-call | tf_op jit(solution)/shard_map/write_out/pallas_call | solution.py:275
Async XLA Ops:
  112.8 4.5 %copy-start = (bf16[2560,2432]{1,0:T(8,128)(2,1)}, bf16[2560,2432]{1,0:T(8,128)(2,1)S(1)}, u32[]{:S(2)}) copy-start(bf16[2560,2432]{1,0:T(8,128)(2,1)S(1)} %get-tuple-element.8.b_v) | copy-start | bytes 37355524
  117.3 0.7 copy-start.1
